TPU v7x, 32 devices: a whole 2x2x4 slice. The times are simulated.
32 devices in a mesh: wave: 16 (over z, x, core), lev: 2 (over y).
Axes of the slice: x: 2, y: 2, z: 4, core: 2. Of those that a mesh axis runs over, the one named last changes fastest.
Arguments:
- spin_tendency: bfloat16 [32, 2, 136, 768], P('wave', None, 'lev'), may hold values from -6 to 6
- spreading_source: bfloat16 [32, 2, 136, 768], P('wave', None, 'lev'), may hold values from -6 to 6
- heat_source: bfloat16 [32, 2, 136, 768], P('wave', None, 'lev'), may hold values from -6 to 6
- helmholtz_inverses: bfloat16 [2, 384, 136, 136], P('lev', 'wave'), may hold values from -0.5 to 0.5
- heat_spreading_coupler: bfloat16 [136, 136], replicated, may hold values from -0.5 to 0.5
- smoothing_strengths: float32 [136], replicated, may hold values from 0.5 to 30
- azimuthal_order_list: int32 [32], P('wave'), may hold values from 0 to 767
Outputs:
- vorticity_new: bfloat16 [32, 2, 136, 768], P('wave', None, 'lev')
- divergence_new: bfloat16 [32, 2, 136, 768], P('wave', None, 'lev')
- temperature_new: bfloat16 [32, 2, 136, 768], P('wave', None, 'lev')
All inputs are finite; a program needn't handle non-finite values.
Results may differ from a plain program's by a relative error of at most 0.0075.
Values may be sent and summed in bfloat16 or wider, within the bound.
A program may use at most 64 MiB of HBM per device.

v0:
```python
import jax
import jax.numpy as jnp
from jax import lax
from jax.sharding import PartitionSpec as P


def damping_table(level_gain, wavenumbers, total_n):
    scaled = (wavenumbers * (wavenumbers + 1)).astype(jnp.float32) / jnp.float32(
        (total_n - 1) * total_n
    )
    return 1.0 / (1.0 + level_gain[:, None] * scaled[None, :] ** 2)


def on_device(
    spin_tendency,
    spreading_source,
    heat_source,
    helmholtz_inverses,
    heat_spreading_coupler,
    smoothing_strengths,
    azimuthal_order_list,
):
    lev_count = lax.axis_size("lev")
    lev_index = lax.axis_index("lev")
    row_count, part_count, lev_local, total_n = spreading_source.shape
    block_n = total_n // lev_count
    layer_count = lev_local * lev_count
    flat_rows = row_count * part_count
    empty_placeholder = jnp.zeros((), jnp.bfloat16)
    wave_count = lax.axis_size("wave")
    local_n = block_n // wave_count
    rhs_div = lax.all_to_all(spreading_source, "lev", split_axis=3, concat_axis=2, tiled=True)
    outgoing = rhs_div.reshape(flat_rows, layer_count, wave_count, local_n).transpose(2, 3, 0, 1)
    outgoing = outgoing.reshape(wave_count, local_n, flat_rows * layer_count)
    columns = lax.all_to_all(outgoing, "wave", split_axis=0, concat_axis=0, tiled=True)
    columns = columns.reshape(wave_count, local_n, flat_rows, layer_count)
    solved_columns = jnp.einsum(
        "jkp,wjcp->wjck", helmholtz_inverses[0], columns, preferred_element_type=jnp.float32
    ).astype(jnp.bfloat16)
    solved_columns = solved_columns.reshape(wave_count, local_n, flat_rows * layer_count)
    returned = lax.all_to_all(solved_columns, "wave", split_axis=0, concat_axis=0, tiled=True)
    answer_fields = returned.reshape(block_n, flat_rows, layer_count).transpose(1, 2, 0)
    coupled = jnp.einsum(
        "om,dms->dos", heat_spreading_coupler, answer_fields, preferred_element_type=jnp.float32
    ).astype(jnp.bfloat16)
    both = jnp.stack([answer_fields, coupled])
    both = lax.all_to_all(both, "lev", split_axis=2, concat_axis=3, tiled=True)
    both = both.reshape(2, row_count, part_count, lev_local, total_n)
    spreading_updated, coupled_out = (both[0], both[1])
    heat_updated = (heat_source.astype(jnp.float32) - coupled_out.astype(jnp.float32)).astype(
        jnp.bfloat16
    )
    level_gain = lax.dynamic_slice_in_dim(smoothing_strengths, lev_index * lev_local, lev_local)
    damping = damping_table(level_gain, jnp.arange(total_n, dtype=jnp.int32), total_n)
    spin_updated = (spin_tendency.astype(jnp.float32) * damping[None, None]).astype(jnp.bfloat16)
    interior_slice = (
        jnp.arange(total_n, dtype=jnp.int32)[None, :] >= azimuthal_order_list[:, None]
    )[:, None, None, :]
    return (
        jnp.where(interior_slice, spin_updated, empty_placeholder),
        jnp.where(interior_slice, spreading_updated, empty_placeholder),
        jnp.where(interior_slice, heat_updated, empty_placeholder),
    )


def solution(mesh):
    return jax.shard_map(
        on_device,
        mesh=mesh,
        in_specs=(
            P("wave", None, "lev", None),
            P("wave", None, "lev", None),
            P("wave", None, "lev", None),
            P("lev", "wave", None, None),
            P(),
            P(),
            P("wave"),
        ),
        out_specs=(
            P("wave", None, "lev", None),
            P("wave", None, "lev", None),
            P("wave", None, "lev", None),
        ),
        check_vma=False,
    )
```

profile of v0, /device:TPU:0, one launch (start us, length us, event | category | flops | bytes accessed | tf_op | source)
XLA Modules:
  0.0 88.3 jit_solution(10291500777090711552)
XLA Ops:
  0.6 0.0 copy-start
  0.6 2.8 %copy.51 = bf16[2,2,68,768]{2,1,0,3:T(2,128)(2,1)S(1)} copy(bf16[2,2,68,768]{3,1,2,0:T(2,128)(2,1)} %param.8) | data formatting | bytes 835584 | tf_op args[1]
  3.5 14.8 %all_to_all.40 = bf16[2,2,68,768]{2,1,0,3:T(2,128)(2,1)S(1)} all-to-all(bf16[2,2,68,768]{2,1,0,3:T(2,128)(2,1)S(1)} %copy.51), channel_id=1, replica_groups=mesh['wave'=16,'lev'=2] {'lev'}, dimensions={3} | all-to-all | bytes 835584 | tf_op jit(solution)/shard_map/all_to_all | solution.py:32
  18.3 0.8 copy.71
  19.2 0.4 reshape.85
  19.6 0.6 copy.53
  20.2 0.5 reshape.86
  20.7 19.6 %all_to_all.41 = bf16[16,24,544]{2,1,0:T(8,128)(2,1)S(1)} all-to-all(bf16[16,24,544]{2,1,0:T(8,128)(2,1)S(1)} %reshape.86), channel_id=1, replica_groups=mesh['wave'=16,'lev'=2] {'wave'}, dimensions={0} | all-to-all | bytes 835584 | tf_op jit(solution)/shard_map/all_to_all | solution.py:35
  40.3 0.5 reshape.87
  40.8 0.0 copy-done
  40.8 0.7 fusion.5
  41.5 0.0 copy-start.3
  41.5 0.4 copy.55
  41.9 1.3 %reshape.88 = bf16[16,24,544]{2,1,0:T(8,128)(2,1)} reshape(bf16[16,24,4,136]{3,2,1,0:T(4,128)(2,1)S(1)} %copy.55) | data formatting | bytes 835584 | tf_op jit(solution)/shard_map/reshape | solution.py:40
  43.2 0.0 copy-start.1
  43.2 4.1 %all-to-all-start.2 = ((bf16[16,24,544]{2,1,0:T(8,128)(2,1)}), bf16[16,24,544]{2,1,0:T(8,128)(2,1)S(1)}, u32[]{:S(2)}, u32[]{:S(2)}) async-start(bf16[16,24,544]{2,1,0:T(8,128)(2,1)} %reshape.88), calls=%async_computation.2 | async-start | bytes 983040 | tf_op jit(solution)/shard_map/all_to_all | solution.py:41
  47.3 0.0 copy-done.3
  47.3 0.1 dynamic_slice.3
  47.4 13.6 %all-to-all-done.2 = bf16[16,24,544]{2,1,0:T(8,128)(2,1)S(1)} async-done(((bf16[16,24,544]{2,1,0:T(8,128)(2,1)}), bf16[16,24,544]{2,1,0:T(8,128)(2,1)S(1)}, u32[]{:S(2)}, u32[]{:S(2)}) %all-to-all-start.2) | async-done | bytes 417824 | tf_op jit(solution)/shard_map/all_to_all | solution.py:41
  61.1 0.5 reshape.89
  61.6 0.9 copy.56
  62.5 0.0 copy-done.1
  62.5 0.3 fusion.8
  62.8 0.1 pad_maximum_fusion
  62.9 0.0 copy-start.2
  62.9 1.2 %copy.57 = bf16[2,4,136,384]{3,1,0,2:T(4,128)(2,1)} copy(bf16[2,4,136,384]{3,2,1,0:T(8,128)(2,1)S(1)} %pad_maximum_fusion) | data formatting | bytes 1671168 | tf_op jit(solution)/shard_map/stack | solution.py:46
  64.1 3.5 %all-to-all-start.3 = ((bf16[2,4,136,384]{3,1,0,2:T(4,128)(2,1)}), bf16[2,4,136,384]{3,1,0,2:T(4,128)(2,1)S(1)}, u32[]{:S(2)}, u32[]{:S(2)}) async-start(bf16[2,4,136,384]{3,1,0,2:T(4,128)(2,1)} %copy.57), calls=%async_computation.3 | async-start | bytes 1671168 | tf_op jit(solution)/shard_map/all_to_all | solution.py:47
  67.6 0.0 copy-done.2
  67.7 0.1 iota_compare_fusion
  67.7 0.8 add_divide_fusion
  68.5 11.0 %all-to-all-done.3 = bf16[2,4,136,384]{3,1,0,2:T(4,128)(2,1)S(1)} async-done(((bf16[2,4,136,384]{3,1,0,2:T(4,128)(2,1)}), bf16[2,4,136,384]{3,1,0,2:T(4,128)(2,1)S(1)}, u32[]{:S(2)}, u32[]{:S(2)}) %all-to-all-start.3) | async-done | bytes 835616 | tf_op jit(solution)/shard_map/all_to_all | solution.py:47
  79.5 0.3 copy.58
  79.8 1.0 %slice_convert_fusion = (f32[1,4,68,2,384]{4,1,2,3,0:T(4,128)S(1)}, bf16[1,4,68,2,384]{4,1,2,3,0:T(4,128)(2,1)}) fusion(bf16[2,4,68,2,384]{4,1,2,3,0:T(4,128)(2,1)S(1)} %bitcast.35), kind=kLoop, calls=%fused_computation.14 | loop fusion | flops 208896 | bytes 2088960 | tf_op jit(solution)/shard_map/convert_element_type | solution.py:50
  80.8 0.4 copy.61
  81.2 0.7 reshape.90
  81.9 1.3 %copy.59 = bf16[1,4,68,2,384]{4,3,2,1,0:T(2,128)(2,1)S(1)} copy(bf16[1,4,68,2,384]{4,1,2,3,0:T(4,128)(2,1)} %get-tuple-element.16) | data formatting | bytes 835584 | tf_op jit(solution)/shard_map/slice | solution.py:49
  83.2 0.3 squeeze.8
  83.5 1.5 %fusion.11 = (bf16[2,2,68,768]{3,2,1,0:T(8,128)(2,1)S(1)}, bf16[2,2,68,768]{3,2,1,0:T(8,128)(2,1)S(1)}, bf16[2,2,68,768]{3,2,1,0:T(8,128)(2,1)S(1)}) fusion(f32[2,2,68,768]{3,2,1,0:T(8,128)S(1)} %reshape.90, bf16[2,2,68,768]{3,1,2,0:T(2,128)(2,1)} %param.9, pred[2,768]{1,0:T(4,128)(4,1)S(1)} %iota_compare_fusion, bf16[2,2,68,768]{3,2,1,0:T(8,128)(2,1)S(1)} %squeeze.8, ...), kind=kLoop, calls=%fused_computation.12 | loop fusion | flops 1880064 | bytes 3552768 | tf_op jit(solution)/shard_map/jit(_where)/select_n | solution.py:62
  85.1 1.1 %copy.64 = bf16[2,2,68,768]{3,1,2,0:T(2,128)(2,1)} copy(bf16[2,2,68,768]{3,2,1,0:T(8,128)(2,1)S(1)} %get-tuple-element.17) | data formatting | bytes 835584
  86.1 1.1 %copy.63 = bf16[2,2,68,768]{3,1,2,0:T(2,128)(2,1)} copy(bf16[2,2,68,768]{3,2,1,0:T(8,128)(2,1)S(1)} %get-tuple-element.18) | data formatting | bytes 835584
  87.2 1.1 %copy.62 = bf16[2,2,68,768]{3,1,2,0:T(2,128)(2,1)} copy(bf16[2,2,68,768]{3,2,1,0:T(8,128)(2,1)S(1)} %get-tuple-element.19) | data formatting | bytes 835584
  (1 shorter events, 0.0 us)
Async XLA Ops:
  0.6 40.2 %copy-start = (bf16[1,24,136,136]{3,2,1,0:T(8,128)(2,1)S(1)}, bf16[1,24,136,136]{3,2,1,0:T(8,128)(2,1)}, u32[]{:S(2)}) copy-start(bf16[1,24,136,136]{3,2,1,0:T(8,128)(2,1)} %param.10) | copy-start | bytes 2663428
  41.5 5.8 %copy-start.3 = (f32[136]{0:T(256)S(1)}, f32[136]{0:T(256)}, u32[]{:S(2)}) copy-start(f32[136]{0:T(256)} %param.12) | copy-start | bytes 1636
  43.2 19.3 %copy-start.1 = (bf16[136,136]{1,0:T(8,128)(2,1)S(1)}, bf16[136,136]{1,0:T(8,128)(2,1)}, u32[]{:S(2)}) copy-start(bf16[136,136]{1,0:T(8,128)(2,1)} %param.11) | copy-start | bytes 110980
  43.2 17.9 %all-to-all-start.2 = ((bf16[16,24,544]{2,1,0:T(8,128)(2,1)}), bf16[16,24,544]{2,1,0:T(8,128)(2,1)S(1)}, u32[]{:S(2)}, u32[]{:S(2)}) async-start(bf16[16,24,544]{2,1,0:T(8,128)(2,1)} %reshape.88), calls=%async_computation.2 | async-start | bytes 983040 | tf_op jit(solution)/shard_map/all_to_all | solution.py:41
  62.9 4.8 %copy-start.2 = (s32[2]{0:T(128)S(1)}, s32[2]{0:T(128)}, u32[]{:S(2)}) copy-start(s32[2]{0:T(128)} %param.13) | copy-start | bytes 28
  64.1 15.4 %all-to-all-start.3 = ((bf16[2,4,136,384]{3,1,0,2:T(4,128)(2,1)}), bf16[2,4,136,384]{3,1,0,2:T(4,128)(2,1)S(1)}, u32[]{:S(2)}, u32[]{:S(2)}) async-start(bf16[2,4,136,384]{3,1,0,2:T(4,128)(2,1)} %copy.57), calls=%async_computation.3 | async-start | bytes 1671168 | tf_op jit(solution)/shard_map/all_to_all | solution.py:47
where the time goes:
time: 88.8 us; the launch traced here: 88.3 us
  blocking collectives  34.4 us (39%)
  waiting for transfers between devices  24.6 us (28%)
  local copies, waits for them, and re-layouts  16.3 us (18%)
  starting transfers between devices  7.66 us (9%)
  other arithmetic  3.5 us (4%)
  matrix products  0.91 us (1%)
    all_to_all x1, blocking collectives, on_device(): lax.all_to_all(outgoing, 'wave', split_axis=0, concat_axis=0, tiled=True)  19.6 us
    all_to_all x1, blocking collectives, on_device(): lax.all_to_all(spreading_source, 'lev', split_axis=3, concat_axis=2, tile...  14.8 us
    all_to_all x1, waiting for transfers between devices, on_device(): lax.all_to_all(solved_columns, 'wave', split_axis=0, concat_axis=0, tiled...  13.6 us
    all_to_all x1, waiting for transfers between devices, on_device(): both = lax.all_to_all(both, 'lev', split_axis=2, concat_axis=3, tiled=True)  11 us
    unnamed x12, local copies, waits for them, and re-layouts  6.1 us
    all_to_all x1, starting transfers between devices, on_device(): lax.all_to_all(solved_columns, 'wave', split_axis=0, concat_axis=0, tiled...  4.12 us
    all_to_all x1, starting transfers between devices, on_device(): both = lax.all_to_all(both, 'lev', split_axis=2, concat_axis=3, tiled=True)  3.54 us
  transfers between devices with their start and end apart: 2, of which 2 were waited for; matrix products, arithmetic and copies ran while one was open for 1% of the time, Pallas kernels for 0%

commit v1 on v0

--- a/solution.py
+++ b/solution.py
@@ -29,7 +29,12 @@
     empty_placeholder = jnp.zeros((), jnp.bfloat16)
     wave_count = lax.axis_size("wave")
     local_n = block_n // wave_count
-    rhs_div = lax.all_to_all(spreading_source, "lev", split_axis=3, concat_axis=2, tiled=True)
+    rhs_div = jnp.concatenate(
+        lax.all_to_all(
+            jnp.stack(jnp.split(spreading_source, lax.axis_size("lev"), axis=3)), "lev", 0, 0
+        ),
+        axis=2,
+    )
     outgoing = rhs_div.reshape(flat_rows, layer_count, wave_count, local_n).transpose(2, 3, 0, 1)
     outgoing = outgoing.reshape(wave_count, local_n, flat_rows * layer_count)
     columns = lax.all_to_all(outgoing, "wave", split_axis=0, concat_axis=0, tiled=True)

time: 88.8 us -> 84.4 us (0.950)
  blocking collectives: 34.4 us -> 30.4 us
  local copies, waits for them, and re-layouts: 16.3 us -> 15.3 us
    all_to_all x1, blocking collectives: 14.8 us -> 10.9 us  [on_device(): lax.all_to_all(jnp.stack(jnp.split(spreading_source, lax.axis_size('lev')...]
    unnamed x12 -> x11, local copies, waits for them, and re-layouts: 6.1 us -> 3.25 us
    another operation x0 -> x2, local copies, waits for them, and re-layouts: none -> 1.89 us  [the longest x1 1.44 us: on_device(): jnp.stack(jnp.split(spreading_source, lax.axis_size('lev'), axis=3))]
where the time goes in v1:
time: 84.4 us; the launch traced here: 83.9 us
  blocking collectives  30.4 us (36%)
  waiting for transfers between devices  24.6 us (29%)
  local copies, waits for them, and re-layouts  15.3 us (18%)
  starting transfers between devices  7.66 us (9%)
  other arithmetic  4.09 us (5%)
  matrix products  0.91 us (1%)
    all_to_all x1, blocking collectives, on_device(): lax.all_to_all(outgoing, 'wave', split_axis=0, concat_axis=0, tiled=True)  19.5 us
    all_to_all x1, waiting for transfers between devices, on_device(): lax.all_to_all(solved_columns, 'wave', split_axis=0, concat_axis=0, tiled...  13.6 us
    all_to_all x1, waiting for transfers between devices, on_device(): both = lax.all_to_all(both, 'lev', split_axis=2, concat_axis=3, tiled=True)  11 us
    all_to_all x1, blocking collectives, on_device(): lax.all_to_all(jnp.stack(jnp.split(spreading_source, lax.axis_size('lev')...  10.9 us
    all_to_all x1, starting transfers between devices, on_device(): lax.all_to_all(solved_columns, 'wave', split_axis=0, concat_axis=0, tiled...  4.12 us
    all_to_all x1, starting transfers between devices, on_device(): both = lax.all_to_all(both, 'lev', split_axis=2, concat_axis=3, tiled=True)  3.54 us
    unnamed x11, local copies, waits for them, and re-layouts  3.25 us
  transfers between devices with their start and end apart: 2, of which 2 were waited for; matrix products, arithmetic and copies ran while one was open for 1% of the time, Pallas kernels for 0%

profile of v1, /device:TPU:0, one launch (start us, length us, event | category | flops | bytes accessed | tf_op | source)
XLA Modules:
  0.0 83.9 jit_solution(10235607830883177280)
XLA Ops:
  0.6 0.0 copy-start
  0.6 1.4 %slice_bitcast_fusion.1 = (bf16[1,2,2,68,384]{4,2,3,1,0:T(2,128)(2,1)S(1)}, bf16[1,2,2,68,384]{4,2,3,1,0:T(2,128)(2,1)S(1)}) fusion(bf16[2,2,68,768]{3,1,2,0:T(2,128)(2,1)} %param.8), kind=kLoop, calls=%fused_computation.18 | loop fusion | bytes 835584 | tf_op jit(solution)/shard_map/stack | solution.py:34
  2.1 0.6 pad_maximum_fusion.1
  2.7 10.9 %all_to_all.30 = bf16[2,2,2,68,384]{4,2,3,1,0:T(2,128)(2,1)S(1)} all-to-all(bf16[2,2,2,68,384]{4,2,3,1,0:T(2,128)(2,1)S(1)} %pad_maximum_fusion.1), channel_id=1, replica_groups=mesh['wave'=16,'lev'=2] {'lev'}, dimensions={0} | all-to-all | bytes 835584 | tf_op jit(solution)/shard_map/all_to_all | solution.py:33
  13.6 1.2 %copy.36 = bf16[2,2,2,68,384]{3,2,4,1,0:T(2,128)(2,1)S(1)} copy(bf16[2,2,2,68,384]{4,1,3,0,2:T(2,128)(2,1)S(1)} %bitcast.38) | data formatting | bytes 835584 | tf_op jit(solution)/shard_map/reshape | solution.py:32
  14.8 0.4 reshape_reshape.3
  15.2 0.6 copy.37
  15.9 0.5 reshape.85
  16.4 19.5 %all_to_all.31 = bf16[16,24,544]{2,1,0:T(8,128)(2,1)S(1)} all-to-all(bf16[16,24,544]{2,1,0:T(8,128)(2,1)S(1)} %reshape.85), channel_id=1, replica_groups=mesh['wave'=16,'lev'=2] {'wave'}, dimensions={0} | all-to-all | bytes 835584 | tf_op jit(solution)/shard_map/all_to_all | solution.py:40
  35.9 0.5 reshape.86
  36.4 0.0 copy-done
  36.4 0.7 fusion.5
  37.1 0.0 copy-start.3
  37.1 0.4 copy.39
  37.5 1.3 %reshape.87 = bf16[16,24,544]{2,1,0:T(8,128)(2,1)} reshape(bf16[16,24,4,136]{3,2,1,0:T(4,128)(2,1)S(1)} %copy.39) | data formatting | bytes 835584 | tf_op jit(solution)/shard_map/reshape | solution.py:45
  38.8 0.0 copy-start.1
  38.8 4.1 %all-to-all-start.2 = ((bf16[16,24,544]{2,1,0:T(8,128)(2,1)}), bf16[16,24,544]{2,1,0:T(8,128)(2,1)S(1)}, u32[]{:S(2)}, u32[]{:S(2)}) async-start(bf16[16,24,544]{2,1,0:T(8,128)(2,1)} %reshape.87), calls=%async_computation.2 | async-start | bytes 983040 | tf_op jit(solution)/shard_map/all_to_all | solution.py:46
  42.9 0.0 copy-done.3
  42.9 0.1 dynamic_slice.3
  43.0 13.6 %all-to-all-done.2 = bf16[16,24,544]{2,1,0:T(8,128)(2,1)S(1)} async-done(((bf16[16,24,544]{2,1,0:T(8,128)(2,1)}), bf16[16,24,544]{2,1,0:T(8,128)(2,1)S(1)}, u32[]{:S(2)}, u32[]{:S(2)}) %all-to-all-start.2) | async-done | bytes 417824 | tf_op jit(solution)/shard_map/all_to_all | solution.py:46
  56.7 0.5 reshape.88
  57.2 0.9 %copy.40 = bf16[384,4,136]{0,2,1:T(8,128)(2,1)S(1)} copy(bf16[384,4,136]{2,1,0:T(4,128)(2,1)S(1)} %reshape.88) | data formatting | bytes 835584 | tf_op jit(solution)/shard_map/reshape | solution.py:47
  58.1 0.0 copy-done.1
  58.1 0.3 fusion.8
  58.3 0.1 pad_maximum_fusion
  58.4 0.0 copy-start.2
  58.5 1.2 %copy.41 = bf16[2,4,136,384]{3,1,0,2:T(4,128)(2,1)} copy(bf16[2,4,136,384]{3,2,1,0:T(8,128)(2,1)S(1)} %pad_maximum_fusion) | data formatting | bytes 1671168 | tf_op jit(solution)/shard_map/stack | solution.py:51
  59.7 3.5 %all-to-all-start.3 = ((bf16[2,4,136,384]{3,1,0,2:T(4,128)(2,1)}), bf16[2,4,136,384]{3,1,0,2:T(4,128)(2,1)S(1)}, u32[]{:S(2)}, u32[]{:S(2)}) async-start(bf16[2,4,136,384]{3,1,0,2:T(4,128)(2,1)} %copy.41), calls=%async_computation.3 | async-start | bytes 1671168 | tf_op jit(solution)/shard_map/all_to_all | solution.py:52
  63.2 0.0 copy-done.2
  63.3 0.1 iota_compare_fusion
  63.3 0.8 add_divide_fusion
  64.1 11.0 %all-to-all-done.3 = bf16[2,4,136,384]{3,1,0,2:T(4,128)(2,1)S(1)} async-done(((bf16[2,4,136,384]{3,1,0,2:T(4,128)(2,1)}), bf16[2,4,136,384]{3,1,0,2:T(4,128)(2,1)S(1)}, u32[]{:S(2)}, u32[]{:S(2)}) %all-to-all-start.3) | async-done | bytes 835616 | tf_op jit(solution)/shard_map/all_to_all | solution.py:52
  75.1 0.3 copy.42
  75.4 1.0 %slice_convert_fusion = (f32[1,4,68,2,384]{4,1,2,3,0:T(4,128)S(1)}, bf16[1,4,68,2,384]{4,1,2,3,0:T(4,128)(2,1)}) fusion(bf16[2,4,68,2,384]{4,1,2,3,0:T(4,128)(2,1)S(1)} %bitcast.36), kind=kLoop, calls=%fused_computation.13 | loop fusion | flops 208896 | bytes 2088960 | tf_op jit(solution)/shard_map/convert_element_type | solution.py:55
  76.4 0.4 copy.45
  76.8 0.7 reshape.89
  77.5 1.3 %copy.43 = bf16[1,4,68,2,384]{4,3,2,1,0:T(2,128)(2,1)S(1)} copy(bf16[1,4,68,2,384]{4,1,2,3,0:T(4,128)(2,1)} %get-tuple-element.13) | data formatting | bytes 835584 | tf_op jit(solution)/shard_map/slice | solution.py:54
  78.8 0.3 squeeze.8
  79.1 1.5 %fusion.11 = (bf16[2,2,68,768]{3,2,1,0:T(8,128)(2,1)S(1)}, bf16[2,2,68,768]{3,2,1,0:T(8,128)(2,1)S(1)}, bf16[2,2,68,768]{3,2,1,0:T(8,128)(2,1)S(1)}) fusion(f32[2,2,68,768]{3,2,1,0:T(8,128)S(1)} %reshape.89, bf16[2,2,68,768]{3,1,2,0:T(2,128)(2,1)} %param.9, pred[2,768]{1,0:T(4,128)(4,1)S(1)} %iota_compare_fusion, bf16[2,2,68,768]{3,2,1,0:T(8,128)(2,1)S(1)} %squeeze.8, ...), kind=kLoop, calls=%fused_computation.11 | loop fusion | flops 1880064 | bytes 3552768 | tf_op jit(solution)/shard_map/jit(_where)/select_n | solution.py:67
  80.6 1.1 %copy.48 = bf16[2,2,68,768]{3,1,2,0:T(2,128)(2,1)} copy(bf16[2,2,68,768]{3,2,1,0:T(8,128)(2,1)S(1)} %get-tuple-element.16) | data formatting | bytes 835584
  81.7 1.1 %copy.47 = bf16[2,2,68,768]{3,1,2,0:T(2,128)(2,1)} copy(bf16[2,2,68,768]{3,2,1,0:T(8,128)(2,1)S(1)} %get-tuple-element.17) | data formatting | bytes 835584
  82.8 1.1 %copy.46 = bf16[2,2,68,768]{3,1,2,0:T(2,128)(2,1)} copy(bf16[2,2,68,768]{3,2,1,0:T(8,128)(2,1)S(1)} %get-tuple-element.18) | data formatting | bytes 835584
  (1 shorter events, 0.0 us)
Async XLA Ops:
  0.6 35.8 %copy-start = (bf16[1,24,136,136]{3,2,1,0:T(8,128)(2,1)S(1)}, bf16[1,24,136,136]{3,2,1,0:T(8,128)(2,1)}, u32[]{:S(2)}) copy-start(bf16[1,24,136,136]{3,2,1,0:T(8,128)(2,1)} %param.10) | copy-start | bytes 2663428
  37.1 5.9 %copy-start.3 = (f32[136]{0:T(256)S(1)}, f32[136]{0:T(256)}, u32[]{:S(2)}) copy-start(f32[136]{0:T(256)} %param.12) | copy-start | bytes 1636
  38.8 19.3 %copy-start.1 = (bf16[136,136]{1,0:T(8,128)(2,1)S(1)}, bf16[136,136]{1,0:T(8,128)(2,1)}, u32[]{:S(2)}) copy-start(bf16[136,136]{1,0:T(8,128)(2,1)} %param.11) | copy-start | bytes 110980
  38.8 17.9 %all-to-all-start.2 = ((bf16[16,24,544]{2,1,0:T(8,128)(2,1)}), bf16[16,24,544]{2,1,0:T(8,128)(2,1)S(1)}, u32[]{:S(2)}, u32[]{:S(2)}) async-start(bf16[16,24,544]{2,1,0:T(8,128)(2,1)} %reshape.87), calls=%async_computation.2 | async-start | bytes 983040 | tf_op jit(solution)/shard_map/all_to_all | solution.py:46
  58.4 4.8 %copy-start.2 = (s32[2]{0:T(128)S(1)}, s32[2]{0:T(128)}, u32[]{:S(2)}) copy-start(s32[2]{0:T(128)} %param.13) | copy-start | bytes 28
  59.7 15.4 %all-to-all-start.3 = ((bf16[2,4,136,384]{3,1,0,2:T(4,128)(2,1)}), bf16[2,4,136,384]{3,1,0,2:T(4,128)(2,1)S(1)}, u32[]{:S(2)}, u32[]{:S(2)}) async-start(bf16[2,4,136,384]{3,1,0,2:T(4,128)(2,1)} %copy.41), calls=%async_computation.3 | async-start | bytes 1671168 | tf_op jit(solution)/shard_map/all_to_all | solution.py:52
